TPU v7x, 256 devices: a whole 4x4x8 slice. The times are simulated.
256 devices in a mesh: copy: 2 (over core), fsdp: 32 (over z, y), tp: 4 (over x).
Axes of the slice: x: 4, y: 4, z: 8, core: 2. Of those that a mesh axis runs over, the one named last changes fastest.
Arguments:
- gradients: float32 [256, 128, 4096], P('copy', 'fsdp', 'tp'), parts along dimension 0, may hold values from -6 to 6
- momentum: float32 [256, 128, 4096], P('copy', 'fsdp', 'tp'), parts along dimension 0, may hold values from -6 to 6
- weights: float32 [256, 128, 4096], P('copy', 'fsdp', 'tp'), parts along dimension 0, may hold values from -0.1875 to 0.1875
Outputs:
- new_weights: float32 [256, 128, 4096], P('copy', 'fsdp', 'tp'), parts along dimension 0
- new_momentum: float32 [256, 128, 4096], P('copy', 'fsdp', 'tp'), parts along dimension 0
There are 2 independent parts, one for each index of `copy`. A program takes and returns all parts, laid end to end along the dimension named above; each array names one. Nothing has to cross between parts.
All inputs are finite; a program needn't handle non-finite values.
Results may differ from a plain program's by a relative error of at most 0.00014.
Values sent between devices are 32-bit elements; how exact they have to be, the bound alone decides.
A program may use at most 64 MiB of HBM per device.

v0:
```python
import jax
import jax.numpy as jnp
from jax import lax
from jax.sharding import PartitionSpec as P

ITERS = 4


hold_rate = 0.95
learn_rate = 0.9
decay_rate = 0.1


def sent_to_all(x, axis):
    length = lax.axis_size(axis)
    return lax.all_to_all(jnp.broadcast_to(x[None], (length, *x.shape)), axis, 0, 0, tiled=True)


def taken_together(x, axis):
    return sent_to_all(x, axis).sum(axis=0)


def shards(gradients, momentum, weights):
    new_momentum = hold_rate * momentum + gradients
    direction = hold_rate * new_momentum + gradients
    moved = lax.all_to_all(direction, "fsdp", split_axis=0, concat_axis=1, tiled=True)
    total = lax.psum(jnp.sum(moved * moved, axis=(1, 2), keepdims=True), "tp")
    iterate = moved * lax.rsqrt(total + 1e-06)
    for step in range(ITERS):
        gram = taken_together(
            jnp.einsum("mik,mjk->mij", iterate, iterate, precision=lax.Precision.HIGHEST), "tp"
        )
        mixed = -4.775 * gram + 2.0315 * jnp.einsum(
            "mij,mjk->mik", gram, gram, precision=lax.Precision.HIGHEST
        )
        iterate = 3.4445 * iterate + jnp.einsum(
            "mij,mjk->mik", mixed, iterate, precision=lax.Precision.HIGHEST
        )
    back = lax.all_to_all(iterate, "fsdp", split_axis=1, concat_axis=0, tiled=True)
    new_weights = (1.0 - learn_rate * decay_rate) * weights - learn_rate * back
    return (new_weights, new_momentum)


def solution(mesh):
    return jax.shard_map(
        shards,
        mesh=mesh,
        in_specs=(P("copy", "fsdp", "tp"), P("copy", "fsdp", "tp"), P("copy", "fsdp", "tp")),
        out_specs=(P("copy", "fsdp", "tp"), P("copy", "fsdp", "tp")),
        check_vma=False,
    )
```

profile of v0, /device:TPU:2, one launch (start us, length us, event | category | flops | bytes accessed | tf_op | source)
XLA Modules:
  0.0 216.3 jit_solution(7391377207697536260)
XLA Ops:
  0.6 4.6 %multiply_add_fusion.4 = (f32[128,4,1024]{2,1,0:T(4,128)S(1)}, f32[128,4,1024]{2,1,0:T(4,128)}) fusion(f32[128,4,1024]{2,1,0:T(4,128)} %param.3, f32[128,4,1024]{2,1,0:T(4,128)} %param.4), kind=kLoop, calls=%fused_computation.7 | loop fusion | flops 2097152 | bytes 8388608 | tf_op jit(solution)/shard_map/add | solution.py:25
  5.3 61.8 %all_to_all.47 = f32[128,4,1024]{2,1,0:T(4,128)S(1)} all-to-all(f32[128,4,1024]{2,1,0:T(4,128)S(1)} %get-tuple-element.2), channel_id=1, replica_groups=mesh['copy'=2,'fsdp'=32,'tp'=4] {'fsdp'}, dimensions={0} | all-to-all | bytes 4194304 | tf_op jit(solution)/shard_map/all_to_all | solution.py:26
  67.0 0.6 multiply_reduce_fusion
  67.7 8.6 %psum.7 = f32[4,1,1]{0,2,1:T(1,128)S(1)} all-reduce(f32[4,1,1]{0,2,1:T(1,128)S(1)} %bitcast.38), channel_id=1, replica_groups=mesh['copy'=2,'fsdp'=32,'tp'=4] {'tp'}, use_global_device_ids=true, to_apply=%region_1.0 | all-reduce | flops 4 | bytes 32 | tf_op jit(solution)/shard_map/psum | solution.py:27
  76.3 1.5 copy_bitcast_fusion
  77.8 2.0 all_to_all.35
  79.8 0.0 copy-start.1
  79.8 2.3 %fusion.2 = f32[4,128,128]{2,1,0:T(8,128)S(1)} fusion(f32[4,128,1024]{2,1,0:T(8,128)S(1)} %all_to_all.35, f32[4]{0:T(128)S(1)} %rsqrt_bitcast_fusion), kind=kOutput, calls=%fused_computation.11 | convolution fusion | flops 805830656 | bytes 2359312 | tf_op jit(solution)/shard_map/mik,mjk->mij/dot_general | solution.py:31
  82.1 0.1 broadcast_in_dim.11
  82.2 14.6 %all_to_all.48 = f32[4,4,128,128]{3,2,1,0:T(8,128)S(1)} all-to-all(f32[4,4,128,128]{3,2,1,0:T(8,128)S(1)} %broadcast_in_dim.11), channel_id=1, replica_groups=mesh['copy'=2,'fsdp'=32,'tp'=4] {'tp'}, dimensions={0} | all-to-all | bytes 2097152 | tf_op jit(solution)/shard_map/all_to_all | solution.py:16
  96.8 0.0 copy-done.1
  96.8 0.1 reduce_sum.46
  96.9 0.4 fusion.9
  97.2 4.3 %multiply_add_fusion.3 = f32[4,128,1024]{2,1,0:T(8,128)S(1)} fusion(f32[4,128,1024]{2,1,0:T(8,128)} %copy-done.1, f32[4,128,128]{2,1,0:T(8,128)S(1)} %fusion.9, f32[4]{0:T(128)S(1)} %rsqrt_bitcast_fusion), kind=kOutput, calls=%fused_computation.5 | convolution fusion | flops 807403520 | bytes 4456464 | tf_op jit(solution)/shard_map/mij,mjk->mik/dot_general | solution.py:36
  101.5 2.0 fusion.12
  103.6 0.1 broadcast_in_dim.12
  103.7 13.3 %all_to_all.49 = f32[4,4,128,128]{3,2,1,0:T(8,128)S(1)} all-to-all(f32[4,4,128,128]{3,2,1,0:T(8,128)S(1)} %broadcast_in_dim.12), channel_id=1, replica_groups=mesh['copy'=2,'fsdp'=32,'tp'=4] {'tp'}, dimensions={0} | all-to-all | bytes 2097152 | tf_op jit(solution)/shard_map/all_to_all | solution.py:16
  117.0 0.1 reduce_sum.47
  117.1 0.4 fusion.8
  117.5 2.0 multiply_add_fusion.2
  119.5 0.0 copy-start
  119.5 2.0 fusion.13
  121.6 0.0 copy-done
  121.6 0.1 broadcast_in_dim.13
  121.7 13.3 %all_to_all.50 = f32[4,4,128,128]{3,2,1,0:T(8,128)S(1)} all-to-all(f32[4,4,128,128]{3,2,1,0:T(8,128)S(1)} %broadcast_in_dim.13), channel_id=1, replica_groups=mesh['copy'=2,'fsdp'=32,'tp'=4] {'tp'}, dimensions={0} | all-to-all | bytes 2097152 | tf_op jit(solution)/shard_map/all_to_all | solution.py:16
  135.0 0.1 reduce_sum.48
  135.1 0.4 fusion.7
  135.4 4.2 %multiply_add_fusion.1 = f32[4,128,1024]{2,1,0:T(8,128)S(1)} fusion(f32[4,128,1024]{2,1,0:T(8,128)} %copy-done, f32[4,128,128]{2,1,0:T(8,128)S(1)} %fusion.7), kind=kOutput, calls=%fused_computation.3 | convolution fusion | flops 806354944 | bytes 4456448 | tf_op jit(solution)/shard_map/mij,mjk->mik/dot_general | solution.py:36
  139.6 2.0 fusion.14
  141.7 0.1 broadcast_in_dim.14
  141.8 13.3 %all_to_all.51 = f32[4,4,128,128]{3,2,1,0:T(8,128)S(1)} all-to-all(f32[4,4,128,128]{3,2,1,0:T(8,128)S(1)} %broadcast_in_dim.14), channel_id=1, replica_groups=mesh['copy'=2,'fsdp'=32,'tp'=4] {'tp'}, dimensions={0} | all-to-all | bytes 2097152 | tf_op jit(solution)/shard_map/all_to_all | solution.py:16
  155.1 0.1 reduce_sum.49
  155.2 0.4 fusion.6
  155.5 2.0 multiply_add_fusion
  157.6 1.4 copy.11
  158.9 52.4 %all_to_all.52 = f32[4,128,1024]{2,0,1:T(4,128)S(1)} all-to-all(f32[4,128,1024]{2,0,1:T(4,128)S(1)} %copy.11), channel_id=1, replica_groups=mesh['copy'=2,'fsdp'=32,'tp'=4] {'fsdp'}, dimensions={1} | all-to-all | bytes 4194304 | tf_op jit(solution)/shard_map/all_to_all | solution.py:39
  211.3 0.7 broadcast_multiply_fusion
  212.0 0.0 copy-start.2
  212.0 1.8 copy.12
  213.8 0.0 copy-done.2
  213.9 2.5 %bitcast_subtract_fusion = f32[128,4,1024]{2,1,0:T(4,128)} fusion(f32[32,4,4,1024]{3,2,1,0:T(4,128)S(1)} %copy.12, f32[128,4,1024]{2,1,0:T(4,128)S(1)} %copy-done.2), kind=kLoop, calls=%fused_computation | loop fusion | flops 1048576 | bytes 6291456 | tf_op jit(solution)/shard_map/sub | solution.py:40
  (1 shorter events, 0.0 us)
Async XLA Ops:
  79.8 17.0 %copy-start.1 = (f32[4,128,1024]{2,1,0:T(8,128)}, f32[4,128,1024]{2,1,0:T(8,128)S(1)}, u32[]{:S(2)}) copy-start(f32[4,128,1024]{2,1,0:T(8,128)S(1)} %all_to_all.35) | copy-start | bytes 6291460
  119.5 2.1 copy-start
  212.0 1.8 copy-start.2
where the time goes:
time: 218 us; the launch traced here: 216 us
  blocking collectives  177 us (81%)
  matrix products  22.4 us (10%)
  other arithmetic  8.7 us (4%)
  local copies, waits for them, and re-layouts  7.09 us (3%)
    all_to_all x1, blocking collectives, shards(): lax.all_to_all(direction, 'fsdp', split_axis=0, concat_axis=1, tiled=True)  61.8 us
    all_to_all x4, blocking collectives, sent_to_all(): lax.all_to_all(jnp.broadcast_to(x[None], (length, *x.shape)), axis, 0, 0,...  54.5 us
    all_to_all x1, blocking collectives, shards(): lax.all_to_all(iterate, 'fsdp', split_axis=1, concat_axis=0, tiled=True)  52.4 us
    dot_general x4, matrix products, shards(): jnp.einsum('mij,mjk->mik', mixed, iterate, precision=lax.Precision.HIGHEST)  12.5 us
    psum x1, blocking collectives, shards(): total = lax.psum(jnp.sum(moved * moved, axis=(1, 2), keepdims=True), 'tp')  8.58 us
    dot_general x4, matrix products, shards(): jnp.einsum('mik,mjk->mij', iterate, iterate, precision=lax.Precision.HIGH...  8.4 us
    add x1, other arithmetic, shards(): direction = hold_rate * new_momentum + gradients  4.62 us

commit v1 on v0

v1 whole, which is shorter than its diff:
```python
import jax
import jax.numpy as jnp
from jax import lax
from jax.sharding import PartitionSpec as P

ITERS = 4


hold_rate = 0.95
learn_rate = 0.9
decay_rate = 0.1


def product(a, b):
    return jnp.einsum("mij,mjk->mik", a, b, precision=lax.Precision.HIGHEST)


def sent_to_all(x, axis):
    length = lax.axis_size(axis)
    return lax.all_to_all(jnp.broadcast_to(x[None], (length, *x.shape)), axis, 0, 0, tiled=True)


def shards(gradients, momentum, weights):
    new_momentum = hold_rate * momentum + gradients
    direction = hold_rate * new_momentum + gradients
    moved = lax.all_to_all(direction, "fsdp", split_axis=0, concat_axis=1, tiled=True)
    gram = sent_to_all(
        jnp.einsum("mik,mjk->mij", moved, moved, precision=lax.Precision.HIGHEST), "tp"
    ).sum(axis=0)
    eye = jnp.eye(gram.shape[-1], dtype=gram.dtype)
    total = jnp.sum(gram * eye, axis=(1, 2), keepdims=True)
    scale = lax.rsqrt(total + 1e-06)
    gram = gram * (scale * scale)
    taken = None
    for step in range(ITERS):
        mixed = 3.4445 * eye - 4.775 * gram + 2.0315 * product(gram, gram)
        taken = mixed if taken is None else product(mixed, taken)
        if step < ITERS - 1:
            gram = product(product(mixed, gram), mixed)
    iterate = product(taken * scale, moved)
    back = lax.all_to_all(iterate, "fsdp", split_axis=1, concat_axis=0, tiled=True)
    new_weights = (1.0 - learn_rate * decay_rate) * weights - learn_rate * back
    return (new_weights, new_momentum)


def solution(mesh):
    return jax.shard_map(
        shards,
        mesh=mesh,
        in_specs=(P("copy", "fsdp", "tp"), P("copy", "fsdp", "tp"), P("copy", "fsdp", "tp")),
        out_specs=(P("copy", "fsdp", "tp"), P("copy", "fsdp", "tp")),
        check_vma=False,
    )
```

time: 218 us -> 161 us (0.74)
  blocking collectives: 177 us -> 117 us
  matrix products: 22.4 us -> 9.17 us
  waiting for transfers between devices: 0 us -> 11.5 us
  starting transfers between devices: 0 us -> 4.83 us
    all_to_all x4 -> x0, blocking collectives: 54.5 us -> none  [sent_to_all(): lax.all_to_all(jnp.broadcast_to(x[None], (length, *x.shape)), axis, 0, 0,...]
    dot_general x12 -> x15, matrix products: 22.4 us -> 9.17 us  [the longest x14 7.12 us: product(): return jnp.einsum('mij,mjk->mik', a, b, precision=lax.Precision.HIGHEST)]
    all_to_all x0 -> x1, waiting for transfers between devices: none -> 11.5 us  [sent_to_all(): lax.all_to_all(jnp.broadcast_to(x[None], (length, *x.shape)), axis, 0, 0,...]
    psum x1 -> x0, blocking collectives: 8.58 us -> none  [shards(): total = lax.psum(jnp.sum(moved * moved, axis=(1, 2), keepdims=True), 'tp')]
    all_to_all x0 -> x1, starting transfers between devices: none -> 4.83 us  [sent_to_all(): lax.all_to_all(jnp.broadcast_to(x[None], (length, *x.shape)), axis, 0, 0,...]
    all_to_all x1, blocking collectives: 52.4 us -> 55.3 us  [shards(): lax.all_to_all(iterate, 'fsdp', split_axis=1, concat_axis=0, tiled=True)]
  transfers between devices with their start and end apart: 0 -> 1, of which waited for: 0 -> 1; matrix products, arithmetic and copies ran while one was open for 0% -> 0% of each run, Pallas kernels for 0% -> 0%
where the time goes in v1:
time: 161 us; the launch traced here: 159 us
  blocking collectives  117 us (73%)
  waiting for transfers between devices  11.5 us (7%)
  matrix products  9.17 us (6%)
  other arithmetic  8.01 us (5%)
  local copies, waits for them, and re-layouts  7.76 us (5%)
  starting transfers between devices  4.83 us (3%)
    all_to_all x1, blocking collectives, shards(): lax.all_to_all(direction, 'fsdp', split_axis=0, concat_axis=1, tiled=True)  61.8 us
    all_to_all x1, blocking collectives, shards(): lax.all_to_all(iterate, 'fsdp', split_axis=1, concat_axis=0, tiled=True)  55.3 us
    all_to_all x1, waiting for transfers between devices, sent_to_all(): lax.all_to_all(jnp.broadcast_to(x[None], (length, *x.shape)), axis, 0, 0,...  11.5 us
    dot_general x14, matrix products, product(): return jnp.einsum('mij,mjk->mik', a, b, precision=lax.Precision.HIGHEST)  7.12 us
    all_to_all x1, starting transfers between devices, sent_to_all(): lax.all_to_all(jnp.broadcast_to(x[None], (length, *x.shape)), axis, 0, 0,...  4.83 us
    add x1, other arithmetic, shards(): direction = hold_rate * new_momentum + gradients  4.62 us
    all_to_all x2, local copies, waits for them, and re-layouts, shards(): lax.all_to_all(direction, 'fsdp', split_axis=0, concat_axis=1, tiled=True)  3.52 us
  transfers between devices with their start and end apart: 1, of which 1 were waited for; matrix products, arithmetic and copies ran while one was open for 0% of the time, Pallas kernels for 0%

profile of v1, /device:TPU:2, one launch (start us, length us, event | category | flops | bytes accessed | tf_op | source)
XLA Modules:
  0.0 159.1 jit_solution(5299643785760654212)
XLA Ops:
  0.6 4.6 %multiply_add_fusion = (f32[128,4,1024]{2,1,0:T(4,128)S(1)}, f32[128,4,1024]{2,1,0:T(4,128)}) fusion(f32[128,4,1024]{2,1,0:T(4,128)} %param.3, f32[128,4,1024]{2,1,0:T(4,128)} %param.4), kind=kLoop, calls=%fused_computation.2 | loop fusion | flops 2097152 | bytes 8388608 | tf_op jit(solution)/shard_map/add | solution.py:25
  5.3 61.8 %all_to_all.32 = f32[128,4,1024]{2,1,0:T(4,128)S(1)} all-to-all(f32[128,4,1024]{2,1,0:T(4,128)S(1)} %get-tuple-element.2), channel_id=1, replica_groups=mesh['copy'=2,'fsdp'=32,'tp'=4] {'fsdp'}, dimensions={0} | all-to-all | bytes 4194304 | tf_op jit(solution)/shard_map/all_to_all | solution.py:26
  67.0 1.5 copy.14
  68.6 2.0 %all_to_all.26 = f32[4,128,1024]{2,1,0:T(8,128)S(1)} reshape(f32[4,32,4,1024]{3,2,1,0:T(4,128)} %bitcast.37) | data formatting | bytes 4194304 | tf_op jit(solution)/shard_map/all_to_all | solution.py:26
  70.6 2.0 %fusion.12 = f32[4,128,128]{2,1,0:T(8,128)S(1)} fusion(f32[4,128,1024]{2,1,0:T(8,128)S(1)} %all_to_all.26), kind=kOutput, calls=%fused_computation.25 | convolution fusion | flops 805306368 | bytes 2359296 | tf_op jit(solution)/shard_map/mik,mjk->mij/dot_general | solution.py:28
  72.6 1.1 broadcast_in_dim.2
  73.7 4.8 %all-to-all-start.1 = ((f32[4,4,128,128]{3,2,1,0:T(8,128)}), f32[4,4,128,128]{3,2,1,0:T(8,128)S(1)}, u32[]{:S(2)}, u32[]{:S(2)}) async-start(f32[4,4,128,128]{3,2,1,0:T(8,128)} %broadcast_in_dim.2), calls=%async_computation.1 | async-start | bytes 2097152 | tf_op jit(solution)/shard_map/all_to_all | solution.py:20
  78.6 11.5 %all-to-all-done.1 = f32[4,4,128,128]{3,2,1,0:T(8,128)S(1)} async-done(((f32[4,4,128,128]{3,2,1,0:T(8,128)}), f32[4,4,128,128]{3,2,1,0:T(8,128)S(1)}, u32[]{:S(2)}, u32[]{:S(2)}) %all-to-all-start.1) | async-done | bytes 1048608 | tf_op jit(solution)/shard_map/all_to_all | solution.py:20
  90.0 0.1 reduce_sum.18
  90.1 0.1 multiply_reduce_fusion
  90.2 0.5 fusion.3
  90.7 0.4 fusion.5
  91.2 0.4 fusion.13
  91.6 0.4 fusion.2
  92.0 0.4 fusion.18
  92.4 0.4 fusion.14
  92.8 0.4 fusion.15
  93.2 0.4 fusion.1
  93.6 0.4 fusion.16
  94.0 0.4 fusion.19
  94.4 0.4 fusion.17
  94.8 0.4 fusion
  95.1 0.4 convolution_multiply_fusion
  95.6 1.9 %fusion.20 = f32[4,128,1024]{2,1,0:T(8,128)S(1)} fusion(f32[4,128,128]{2,1,0:T(8,128)S(1)} %convolution_multiply_fusion, f32[4,128,1024]{2,1,0:T(8,128)S(1)} %all_to_all.26), kind=kOutput, calls=%fused_computation.33 | convolution fusion | flops 805306368 | bytes 4456448 | tf_op jit(solution)/shard_map/mij,mjk->mik/dot_general | solution.py:15
  97.5 1.4 copy.11
  98.8 55.3 %all_to_all.33 = f32[4,128,1024]{2,0,1:T(4,128)S(1)} all-to-all(f32[4,128,1024]{2,0,1:T(4,128)S(1)} %copy.11), channel_id=1, replica_groups=mesh['copy'=2,'fsdp'=32,'tp'=4] {'fsdp'}, dimensions={1} | all-to-all | bytes 4194304 | tf_op jit(solution)/shard_map/all_to_all | solution.py:41
  154.1 0.7 broadcast_multiply_fusion
  154.8 0.0 copy-start
  154.8 1.8 %copy.12 = f32[32,4,4,1024]{3,2,1,0:T(4,128)S(1)} copy(f32[32,4,4,1024]{3,1,2,0:T(4,128)S(1)} %bitcast.38) | data formatting | bytes 4194304 | tf_op jit(solution)/shard_map/mul | solution.py:42
  156.6 0.0 copy-done
  156.6 2.5 %bitcast_subtract_fusion = f32[128,4,1024]{2,1,0:T(4,128)} fusion(f32[32,4,4,1024]{3,2,1,0:T(4,128)S(1)} %copy.12, f32[128,4,1024]{2,1,0:T(4,128)S(1)} %copy-done), kind=kLoop, calls=%fused_computation | loop fusion | flops 1048576 | bytes 6291456 | tf_op jit(solution)/shard_map/sub | solution.py:42
  (3 shorter events, 0.0 us)
Async XLA Ops:
  73.7 16.3 %all-to-all-start.1 = ((f32[4,4,128,128]{3,2,1,0:T(8,128)}), f32[4,4,128,128]{3,2,1,0:T(8,128)S(1)}, u32[]{:S(2)}, u32[]{:S(2)}) async-start(f32[4,4,128,128]{3,2,1,0:T(8,128)} %broadcast_in_dim.2), calls=%async_computation.1 | async-start | bytes 2097152 | tf_op jit(solution)/shard_map/all_to_all | solution.py:20
  154.8 1.8 %copy-start = (f32[128,4,1024]{2,1,0:T(4,128)S(1)}, f32[128,4,1024]{2,1,0:T(4,128)}, u32[]{:S(2)}) copy-start(f32[128,4,1024]{2,1,0:T(4,128)} %param.5) | copy-start | bytes 6291460

commit v2 on v0

v2 whole, which is shorter than its diff:
```python
import jax
import jax.numpy as jnp
from jax import lax
from jax.experimental import pallas as pl
from jax.experimental.pallas import tpu as pltpu
from jax.sharding import PartitionSpec as P

ITERS = 4


hold_rate = 0.95
learn_rate = 0.9
decay_rate = 0.1

MESH = pl.DeviceIdType.MESH
HIGHEST = lax.Precision.HIGHEST


def dot(a, b, contract=((1,), (0,))):
    return lax.dot_general(
        a, b, (contract, ((), ())), precision=HIGHEST, preferred_element_type=jnp.float32
    )


def partner(me, i):
    j = i // 4
    dz = lax.rem(8 + (2 * lax.rem(j, 2) - 1) * ((j + 1) // 2), 8)
    z = lax.rem(me // 4 + dz, 8)
    y = lax.rem(lax.rem(me, 4) + lax.rem(i, 4), 4)
    return z * 4 + y


def swapped(a, b):
    upper = lax.broadcasted_iota(jnp.int32, a.shape, 0) < 4
    return (
        jnp.where(upper, a, pltpu.roll(b, 4, 0)),
        jnp.where(upper, pltpu.roll(a, 4, 0), b),
    )


def kernel(
    g_hbm, m_hbm, w_hbm, new_w_hbm, new_m_hbm,
    g, m, w, new_m, out, away, there, home, back, mats, gram, grams,
    load_sem, w_sem, store_sem, w_out_sem, away_send, away_recv, home_send, home_recv, gram_send, gram_recv,
):
    fsdp = lax.axis_size("fsdp")
    tp = lax.axis_size("tp")
    me = lax.axis_index("fsdp")
    col = lax.axis_index("tp")

    barrier = pltpu.get_barrier_semaphore()

    @pl.loop(1, fsdp)
    def _(i):
        pl.semaphore_signal(barrier, inc=1, device_id={"fsdp": partner(me, i)}, device_id_type=MESH)

    @pl.loop(1, tp)
    def _(i):
        pl.semaphore_signal(
            barrier, inc=1, device_id={"tp": lax.rem(col + i, tp)}, device_id_type=MESH
        )

    load_g = pltpu.make_async_copy(g_hbm, g, load_sem.at[0])
    load_m = pltpu.make_async_copy(m_hbm, m, load_sem.at[1])
    load_w = pltpu.make_async_copy(w_hbm, w, w_sem)
    load_g.start()
    load_m.start()
    load_w.start()
    load_g.wait()
    load_m.wait()

    @pl.loop(0, fsdp)
    def _(d):
        for k in range(4):
            grad = g[d, k]
            momentum = hold_rate * m[d, k] + grad
            new_m[d, k] = momentum
            away[k // 2, d, pl.ds(4 * (k % 2), 4), :] = hold_rate * momentum + grad

    store_m = pltpu.make_async_copy(new_m, new_m_hbm, store_sem)
    store_m.start()
    pl.semaphore_wait(barrier, fsdp - 1 + tp - 1)

    for c in range(2):
        @pl.loop(1, fsdp)
        def _(i):
            d = partner(me, i)
            pltpu.make_async_remote_copy(
                src_ref=away.at[c, d],
                dst_ref=there.at[c, me],
                send_sem=away_send.at[c],
                recv_sem=away_recv.at[c],
                device_id={"fsdp": d},
                device_id_type=MESH,
            ).start()

        there[c, me] = away[c, me]

    for c in range(2):
        others = there.at[c, pl.ds(0, fsdp - 1)]
        pltpu.make_async_copy(others, others, away_recv.at[c]).wait()

        @pl.loop(0, fsdp // 2)
        def _(j):
            first, second = swapped(there[c, 2 * j], there[c, 2 * j + 1])
            rows = pl.ds(pl.multiple_of(8 * j, 8), 8)
            mats[0, rows, :] = first
            mats[1, rows, :] = second

        for k in range(2):
            x = mats[k]
            gram[c, k] = dot(x, x, ((1,), (1,)))

        @pl.loop(1, tp)
        def _(i):
            pltpu.make_async_remote_copy(
                src_ref=gram.at[c],
                dst_ref=grams.at[c, col],
                send_sem=gram_send.at[c],
                recv_sem=gram_recv.at[c],
                device_id={"tp": lax.rem(col + i, tp)},
                device_id_type=MESH,
            ).start()

        grams[c, col] = gram[c]
        others = grams.at[c, pl.ds(0, tp - 1)]
        pltpu.make_async_copy(others, others, gram_recv.at[c]).wait()

        shape = gram.shape[2:]
        eye = (
            lax.broadcasted_iota(jnp.int32, shape, 0) == lax.broadcasted_iota(jnp.int32, shape, 1)
        ).astype(jnp.float32)
        takens = []
        for k in range(2):
            a = (grams[c, 0, k] + grams[c, 1, k]) + (grams[c, 2, k] + grams[c, 3, k])
            total = jnp.sum(jnp.sum(a * eye, axis=1, keepdims=True), axis=0, keepdims=True)
            scale = lax.rsqrt(total + 1e-06)
            a = a * (scale * scale)
            taken = None
            for step in range(ITERS):
                mixed = 3.4445 * eye - 4.775 * a + 2.0315 * dot(a, a)
                taken = mixed if taken is None else dot(mixed, taken)
                if step < ITERS - 1:
                    a = dot(dot(mixed, a), mixed)
            takens.append(taken * scale)
        for k in range(2):
            mats[k] = dot(takens[k], mats[k])

        @pl.loop(0, fsdp // 2)
        def _(j):
            rows = pl.ds(pl.multiple_of(8 * j, 8), 8)
            first, second = swapped(mats[0, rows, :], mats[1, rows, :])
            home[c, 2 * j] = first
            home[c, 2 * j + 1] = second

        @pl.loop(1, fsdp)
        def _(i):
            d = partner(me, i)
            pltpu.make_async_remote_copy(
                src_ref=home.at[c, d],
                dst_ref=back.at[c, me],
                send_sem=home_send.at[c],
                recv_sem=home_recv.at[c],
                device_id={"fsdp": d},
                device_id_type=MESH,
            ).start()

        back[c, me] = home[c, me]

    load_w.wait()
    for c in range(2):
        others = back.at[c, pl.ds(0, fsdp - 1)]
        pltpu.make_async_copy(others, others, home_recv.at[c]).wait()

        @pl.loop(0, fsdp)
        def _(d):
            for k in range(2):
                out[d, 2 * c + k] = (1.0 - learn_rate * decay_rate) * w[d, 2 * c + k] - learn_rate * back[
                    c, d, pl.ds(4 * k, 4), :
                ]

        pltpu.make_async_copy(
            out.at[:, pl.ds(2 * c, 2)], new_w_hbm.at[:, pl.ds(2 * c, 2)], w_out_sem.at[c]
        ).start()

    for c in range(2):
        pltpu.make_async_copy(
            out.at[:, pl.ds(2 * c, 2)], new_w_hbm.at[:, pl.ds(2 * c, 2)], w_out_sem.at[c]
        ).wait()
        sent = away.at[c, pl.ds(0, fsdp - 1)]
        pltpu.make_async_copy(sent, sent, away_send.at[c]).wait()
        pltpu.make_async_copy(sent, sent, home_send.at[c]).wait()
        sent = grams.at[c, pl.ds(0, tp - 1)]
        pltpu.make_async_copy(sent, sent, gram_send.at[c]).wait()
    store_m.wait()


def shards(gradients, momentum, weights):
    mats, side, wide = gradients.shape
    fsdp = lax.axis_size("fsdp")
    tp = lax.axis_size("tp")
    shape = (fsdp, mats // fsdp, side, wide)
    rows = side * fsdp
    f32 = jnp.float32
    block = pltpu.VMEM(shape, f32)
    tiles = pltpu.VMEM((2, fsdp, 2 * side, wide), f32)
    sem = pltpu.SemaphoreType.DMA
    new_weights, new_momentum = pl.pallas_call(
        kernel,
        out_shape=[jax.ShapeDtypeStruct(shape, f32)] * 2,
        in_specs=[pl.BlockSpec(memory_space=pl.ANY)] * 3,
        out_specs=[pl.BlockSpec(memory_space=pl.ANY)] * 2,
        scratch_shapes=[
            block, block, block, block, block, tiles, tiles, tiles, tiles,
            pltpu.VMEM((2, rows, wide), f32),
            pltpu.VMEM((2, 2, rows, rows), f32),
            pltpu.VMEM((2, tp, 2, rows, rows), f32),
            sem((2,)), sem, sem, sem((2,)), sem((2,)), sem((2,)), sem((2,)), sem((2,)), sem((2,)), sem((2,)),
        ],
        compiler_params=pltpu.CompilerParams(
            collective_id=0, has_side_effects=True, vmem_limit_bytes=48 * 1024 * 1024
        ),
        name="update",
    )(gradients.reshape(shape), momentum.reshape(shape), weights.reshape(shape))
    return new_weights.reshape(gradients.shape), new_momentum.reshape(gradients.shape)


def solution(mesh):
    return jax.shard_map(
        shards,
        mesh=mesh,
        in_specs=(P("copy", "fsdp", "tp"), P("copy", "fsdp", "tp"), P("copy", "fsdp", "tp")),
        out_specs=(P("copy", "fsdp", "tp"), P("copy", "fsdp", "tp")),
        check_vma=False,
    )
```

time: 218 us -> 108 us (0.50)
  blocking collectives: 177 us -> 0 us
  Pallas kernels: 0 us -> 103 us
  matrix products: 22.4 us -> 0 us
  other arithmetic: 8.7 us -> 0 us
  local copies, waits for them, and re-layouts: 7.09 us -> 2.64 us
    all_to_all x6 -> x0, blocking collectives: 169 us -> none  [the longest x1 61.8 us: shards(): lax.all_to_all(direction, 'fsdp', split_axis=0, concat_axis=1, tiled=True)]
    pallas_call x0 -> x1, Pallas kernels: none -> 103 us  [shards(): pl.pallas_call(kernel, out_shape=[jax.ShapeDtypeStruct(shape, f32)] * 2,...]
    dot_general x12 -> x0, matrix products: 22.4 us -> none  [the longest x4 12.5 us: shards(): jnp.einsum('mij,mjk->mik', mixed, iterate, precision=lax.Precision.HIGHEST)]
    psum x1 -> x0, blocking collectives: 8.58 us -> none  [shards(): total = lax.psum(jnp.sum(moved * moved, axis=(1, 2), keepdims=True), 'tp')]
    add x1 -> x0, other arithmetic: 4.62 us -> none  [shards(): direction = hold_rate * new_momentum + gradients]
    all_to_all x2 -> x0, local copies, waits for them, and re-layouts: 3.52 us -> none  [shards(): lax.all_to_all(direction, 'fsdp', split_axis=0, concat_axis=1, tiled=True)]
    unnamed x6 -> x2, local copies, waits for them, and re-layouts: 0.02 us -> 2.64 us
    sub x1 -> x0, other arithmetic: 2.48 us -> none  [shards(): new_weights = (1.0 - learn_rate * decay_rate) * weights - learn_rate * back]
where the time goes in v2:
time: 108 us; the launch traced here: 106 us
  Pallas kernels  103 us (95%)
  local copies, waits for them, and re-layouts  2.64 us (2%)
    pallas_call x1, Pallas kernels, shards(): pl.pallas_call(kernel, out_shape=[jax.ShapeDtypeStruct(shape, f32)] * 2,...  103 us
    unnamed x2, local copies, waits for them, and re-layouts  2.64 us

profile of v2, /device:TPU:2, one launch (start us, length us, event | category | flops | bytes accessed | tf_op | source)
XLA Modules:
  0.0 106.5 jit_solution(8396393617223037003)
XLA Ops:
  0.6 103.2 %update.1 = (f32[32,4,4,1024]{3,2,1,0:T(4,128)S(1)}, f32[32,4,4,1024]{3,2,1,0:T(4,128)S(1)}) custom-call(f32[32,4,4,1024]{3,2,1,0:T(4,128)} %bitcast.7, f32[32,4,4,1024]{3,2,1,0:T(4,128)} %bitcast.8, f32[32,4,4,1024]{3,2,1,0:T(4,128)} %bitcast.9), custom_call_target="tpu_custom_call" | custom-call | tf_op jit(solution)/shard_map/update/pallas_call | solution.py:208
  103.9 1.3 %copy.7 = f32[128,4,1024]{2,1,0:T(4,128)} copy(f32[128,4,1024]{2,1,0:T(4,128)S(1)} %bitcast.6) | data formatting | bytes 4194304
  105.2 1.3 %copy.8 = f32[128,4,1024]{2,1,0:T(4,128)} copy(f32[128,4,1024]{2,1,0:T(4,128)S(1)} %bitcast.5) | data formatting | bytes 4194304

commit v3 on v0

v3 whole, which is shorter than its diff:
```python
import jax
import jax.numpy as jnp
from jax import lax
from jax.experimental import pallas as pl
from jax.experimental.pallas import tpu as pltpu
from jax.sharding import PartitionSpec as P

ITERS = 4


hold_rate = 0.95
learn_rate = 0.9
decay_rate = 0.1

ZS, YS = 8, 4
OUTWARD = (1, 7, 0, 2, 6, 3, 5, 4)
MESH = pl.DeviceIdType.MESH
HIGHEST = lax.Precision.HIGHEST


def dot(a, b, contract=((1,), (0,))):
    return lax.dot_general(
        a, b, (contract, ((), ())), precision=HIGHEST, preferred_element_type=jnp.float32
    )


def send(src, dst, send_sem, recv_sem, device):
    pltpu.make_async_remote_copy(
        src_ref=src, dst_ref=dst, send_sem=send_sem, recv_sem=recv_sem, device_id=device, device_id_type=MESH
    ).start()


def wait(ref, sem):
    pltpu.make_async_copy(ref, ref, sem).wait()


def swapped(a, b):
    upper = lax.broadcasted_iota(jnp.int32, a.shape, 0) < 4
    return (
        jnp.where(upper, a, pltpu.roll(b, 4, 0)),
        jnp.where(upper, pltpu.roll(a, 4, 0), b),
    )


def iterated(grams):
    shape = grams[0].shape
    eye = (
        lax.broadcasted_iota(jnp.int32, shape, 0) == lax.broadcasted_iota(jnp.int32, shape, 1)
    ).astype(jnp.float32)
    scales = [
        lax.rsqrt(jnp.sum(jnp.sum(a * eye, axis=1, keepdims=True), axis=0, keepdims=True) + 1e-06)
        for a in grams
    ]
    grams = [a * (scale * scale) for a, scale in zip(grams, scales)]
    takens = None
    for step in range(ITERS):
        mixed = [3.4445 * eye - 4.775 * a + 2.0315 * dot(a, a) for a in grams]
        if step < ITERS - 1:
            halves = [dot(m, a) for m, a in zip(mixed, grams)]
        takens = mixed if takens is None else [dot(m, t) for m, t in zip(mixed, takens)]
        if step < ITERS - 1:
            grams = [dot(h, m) for h, m in zip(halves, mixed)]
    return [t * scale for t, scale in zip(takens, scales)]


def kernel(
    g_hbm, m_hbm, w_hbm, new_w, new_m,
    g, m, w, away, there, home, back, mats, gram, grams,
    load_sem, w_sem, away_send, away_recv, home_send, home_recv, gram_send, gram_recv, ready,
):
    fsdp = lax.axis_size("fsdp")
    tp = lax.axis_size("tp")
    me = lax.axis_index("fsdp")
    col = lax.axis_index("tp")
    core = lax.axis_index("copy")
    own_y = lax.rem(me, YS)
    planes = [lax.rem(me // YS + k, ZS) * YS for k in range(ZS)]
    ys = [lax.rem(own_y + k, YS) for k in range(YS)]
    shifted = [lax.rem(own_y + core + k, YS) for k in range(YS)]

    def partners(dz):
        if dz == 0:
            return [planes[0] + ys[k] for k in range(1, YS)]
        return [planes[dz] + shifted[(k + (2 if dz > ZS // 2 else 0)) % YS] for k in range(YS)]

    def load(dz):
        rows = pl.ds(planes[dz], YS)
        return [
            pltpu.make_async_copy(x.at[rows], y.at[rows], load_sem.at[dz, n])
            for n, (x, y) in enumerate(((g_hbm, g), (m_hbm, m)))
        ]

    def direct(dz):
        for copy in load(dz):
            copy.wait()

        @pl.loop(0, YS)
        def _(y):
            d = planes[dz] + y
            for k in range(4):
                grad = g[d, k]
                momentum = hold_rate * m[d, k] + grad
                new_m[d, k] = momentum
                away[k // 2, d, pl.ds(4 * (k % 2), 4), :] = hold_rate * momentum + grad

    def send_away(c, dz):
        for d in partners(dz):
            send(away.at[c, d], there.at[c, me], away_send.at[c], away_recv.at[c], {"fsdp": d})

    def tell(n):
        for dz in (1, ZS - 1):
            pl.semaphore_signal(
                ready.at[n], inc=1, device_id={"fsdp": planes[dz] + own_y}, device_id_type=MESH
            )

    barrier = pltpu.get_barrier_semaphore()
    for dz in (1, ZS - 1, 0):
        for k in range(YS):
            if dz or k:
                pl.semaphore_signal(
                    barrier, inc=1, device_id={"fsdp": planes[dz] + ys[k]}, device_id_type=MESH
                )
    for k in range(1, 4):
        pl.semaphore_signal(barrier, inc=1, device_id={"tp": lax.rem(col + k, tp)}, device_id_type=MESH)

    for dz in OUTWARD:
        for copy in load(dz):
            copy.start()
    for dz in (1, ZS - 1, 0):
        direct(dz)

    pl.semaphore_wait(barrier, 3 * YS - 1 + tp - 1)
    tell(0)
    for c in range(2):
        for dz in (1, ZS - 1):
            send_away(c, dz)
        if c == 0:
            send_away(c, 0)
    for n in range(2):
        for dz in (n + 2, ZS - 2 - n):
            direct(dz)
        pl.semaphore_wait(ready.at[n], 2)
        tell(n + 1)
        for dz in (n + 2, ZS - 2 - n):
            send_away(0, dz)
    direct(4)
    pl.semaphore_wait(ready.at[2], 2)
    send_away(0, 4)
    for dz in (4, 5, 3, 6, 2, 0):
        send_away(1, dz)
    load_w = pltpu.make_async_copy(w_hbm, w, w_sem)
    load_w.start()
    for c in range(2):
        there[c, me] = away[c, me]

    @pl.loop(0, 2)
    def _(c):
        wait(there.at[c, pl.ds(0, fsdp - 1)], away_recv.at[c])

        @pl.loop(0, fsdp // 2)
        def _(j):
            first, second = swapped(there[c, 2 * j], there[c, 2 * j + 1])
            rows = pl.ds(pl.multiple_of(8 * j, 8), 8)
            mats[0, rows, :] = first
            mats[1, rows, :] = second

        for k in range(2):
            x = mats[k]
            gram[c, k] = dot(x, x, ((1,), (1,)))
        for k in range(1, 4):
            send(gram.at[c], grams.at[c, col], gram_send.at[c], gram_recv.at[c], {"tp": lax.rem(col + k, tp)})
        grams[c, col] = gram[c]
        wait(grams.at[c, pl.ds(0, tp - 1)], gram_recv.at[c])

        takens = iterated(
            [(grams[c, 0, k] + grams[c, 1, k]) + (grams[c, 2, k] + grams[c, 3, k]) for k in range(2)]
        )
        for k in range(2):
            mats[k] = dot(takens[k], mats[k])

        @pl.loop(0, fsdp // 2)
        def _(j):
            rows = pl.ds(pl.multiple_of(8 * j, 8), 8)
            first, second = swapped(mats[0, rows, :], mats[1, rows, :])
            home[c, 2 * j] = first
            home[c, 2 * j + 1] = second

        for dz in (0, 4, 5, 3, 6, 2, 7, 1):
            for d in partners(dz):
                send(home.at[c, d], back.at[c, me], home_send.at[c], home_recv.at[c], {"fsdp": d})
        back[c, me] = home[c, me]

    load_w.wait()
    for c in range(2):
        wait(back.at[c, pl.ds(0, fsdp - 1)], home_recv.at[c])

        @pl.loop(0, fsdp)
        def _(d):
            for k in range(2):
                new_w[d, 2 * c + k] = (1.0 - learn_rate * decay_rate) * w[d, 2 * c + k] - learn_rate * back[
                    c, d, pl.ds(4 * k, 4), :
                ]

    for c in range(2):
        wait(away.at[c, pl.ds(0, fsdp - 1)], away_send.at[c])
        wait(home.at[c, pl.ds(0, fsdp - 1)], home_send.at[c])
        wait(grams.at[c, pl.ds(0, tp - 1)], gram_send.at[c])


def shards(gradients, momentum, weights):
    mats, side, wide = gradients.shape
    fsdp = lax.axis_size("fsdp")
    tp = lax.axis_size("tp")
    shape = (fsdp, mats // fsdp, side, wide)
    rows = side * fsdp
    f32 = jnp.float32
    block = pltpu.VMEM(shape, f32)
    tiles = pltpu.VMEM((2, fsdp, 2 * side, wide), f32)
    sem = pltpu.SemaphoreType.DMA
    new_weights, new_momentum = pl.pallas_call(
        kernel,
        out_shape=[jax.ShapeDtypeStruct(shape, f32)] * 2,
        in_specs=[pl.BlockSpec(memory_space=pl.ANY)] * 3,
        out_specs=[pl.BlockSpec(memory_space=pltpu.VMEM)] * 2,
        scratch_shapes=[
            block, block, block, tiles, tiles, tiles, tiles,
            pltpu.VMEM((2, rows, wide), f32),
            pltpu.VMEM((2, 2, rows, rows), f32),
            pltpu.VMEM((2, tp, 2, rows, rows), f32),
            sem((ZS, 2)), sem, sem((2,)), sem((2,)), sem((2,)), sem((2,)), sem((2,)), sem((2,)),
            pltpu.SemaphoreType.REGULAR((3,)),
        ],
        compiler_params=pltpu.CompilerParams(
            collective_id=0, has_side_effects=True, vmem_limit_bytes=48 * 1024 * 1024
        ),
        name="update",
    )(gradients.reshape(shape), momentum.reshape(shape), weights.reshape(shape))
    return new_weights.reshape(gradients.shape), new_momentum.reshape(gradients.shape)


def solution(mesh):
    return jax.shard_map(
        shards,
        mesh=mesh,
        in_specs=(P("copy", "fsdp", "tp"), P("copy", "fsdp", "tp"), P("copy", "fsdp", "tp")),
        out_specs=(P("copy", "fsdp", "tp"), P("copy", "fsdp", "tp")),
        check_vma=False,
    )
```

time: 218 us -> 105 us (0.48)
  blocking collectives: 177 us -> 0 us
  Pallas kernels: 0 us -> 102 us
  matrix products: 22.4 us -> 0 us
  other arithmetic: 8.7 us -> 0 us
  local copies, waits for them, and re-layouts: 7.09 us -> 2.64 us
    all_to_all x6 -> x0, blocking collectives: 169 us -> none  [the longest x1 61.8 us: shards(): lax.all_to_all(direction, 'fsdp', split_axis=0, concat_axis=1, tiled=True)]
    pallas_call x0 -> x1, Pallas kernels: none -> 102 us  [shards(): pl.pallas_call(kernel, out_shape=[jax.ShapeDtypeStruct(shape, f32)] * 2,...]
    dot_general x12 -> x0, matrix products: 22.4 us -> none  [the longest x4 12.5 us: shards(): jnp.einsum('mij,mjk->mik', mixed, iterate, precision=lax.Precision.HIGHEST)]
    psum x1 -> x0, blocking collectives: 8.58 us -> none  [shards(): total = lax.psum(jnp.sum(moved * moved, axis=(1, 2), keepdims=True), 'tp')]
    add x1 -> x0, other arithmetic: 4.62 us -> none  [shards(): direction = hold_rate * new_momentum + gradients]
    all_to_all x2 -> x0, local copies, waits for them, and re-layouts: 3.52 us -> none  [shards(): lax.all_to_all(direction, 'fsdp', split_axis=0, concat_axis=1, tiled=True)]
    unnamed x6 -> x2, local copies, waits for them, and re-layouts: 0.02 us -> 2.64 us
    sub x1 -> x0, other arithmetic: 2.48 us -> none  [shards(): new_weights = (1.0 - learn_rate * decay_rate) * weights - learn_rate * back]
where the time goes in v3:
time: 105 us
  Pallas kernels  102 us (97%)
  local copies, waits for them, and re-layouts  2.64 us (3%)
    pallas_call x1, Pallas kernels, shards(): pl.pallas_call(kernel, out_shape=[jax.ShapeDtypeStruct(shape, f32)] * 2,...  102 us
    unnamed x2, local copies, waits for them, and re-layouts  2.64 us

profile of v3, /device:TPU:2, one launch (start us, length us, event | category | flops | bytes accessed | tf_op | source)
XLA Modules:
  0.0 104.9 jit_solution(12408364592064156461)
XLA Ops:
  0.6 101.6 %update.1 = (f32[32,4,4,1024]{3,2,1,0:T(4,128)S(1)}, f32[32,4,4,1024]{3,2,1,0:T(4,128)S(1)}) custom-call(f32[32,4,4,1024]{3,2,1,0:T(4,128)} %bitcast.7, f32[32,4,4,1024]{3,2,1,0:T(4,128)} %bitcast.8, f32[32,4,4,1024]{3,2,1,0:T(4,128)} %bitcast.9), custom_call_target="tpu_custom_call" | custom-call | tf_op jit(solution)/shard_map/update/pallas_call | solution.py:220
  102.2 1.3 %copy.7 = f32[128,4,1024]{2,1,0:T(4,128)} copy(f32[128,4,1024]{2,1,0:T(4,128)S(1)} %bitcast.6) | data formatting | bytes 4194304
  103.5 1.3 %copy.8 = f32[128,4,1024]{2,1,0:T(4,128)} copy(f32[128,4,1024]{2,1,0:T(4,128)S(1)} %bitcast.5) | data formatting | bytes 4194304

commit v4 on v3

--- a/solution.py
+++ b/solution.py
@@ -205,6 +205,17 @@
         wait(away.at[c, pl.ds(0, fsdp - 1)], away_send.at[c])
         wait(home.at[c, pl.ds(0, fsdp - 1)], home_send.at[c])
         wait(grams.at[c, pl.ds(0, tp - 1)], gram_send.at[c])
+
+
+def stored(a, b, a_out, b_out, sems):
+    copies = [
+        pltpu.make_async_copy(a, a_out, sems.at[0]),
+        pltpu.make_async_copy(b, b_out, sems.at[1]),
+    ]
+    for copy in copies:
+        copy.start()
+    for copy in copies:
+        copy.wait()
 
 
 def shards(gradients, momentum, weights):
@@ -235,6 +246,15 @@
         ),
         name="update",
     )(gradients.reshape(shape), momentum.reshape(shape), weights.reshape(shape))
+    new_weights, new_momentum = pl.pallas_call(
+        stored,
+        out_shape=[jax.ShapeDtypeStruct(shape, f32)] * 2,
+        in_specs=[pl.BlockSpec(memory_space=pl.ANY)] * 2,
+        out_specs=[pl.BlockSpec(memory_space=pl.ANY)] * 2,
+        scratch_shapes=[sem((2,))],
+        compiler_params=pltpu.CompilerParams(vmem_limit_bytes=1024 * 1024),
+        name="stored",
+    )(new_weights, new_momentum)
     return new_weights.reshape(gradients.shape), new_momentum.reshape(gradients.shape)
 
 

time: 105 us -> 104 us (level)
  local copies, waits for them, and re-layouts: 2.64 us -> 0 us
  Pallas kernels: 102 us -> 104 us
    unnamed x2 -> x0, local copies, waits for them, and re-layouts: 2.64 us -> none
    pallas_call x0 -> x1, Pallas kernels: none -> 2.03 us  [shards(): pl.pallas_call(stored, out_shape=[jax.ShapeDtypeStruct(shape, f32)] * 2,...]
where the time goes in v4:
time: 104 us
  Pallas kernels  104 us (100%)
    pallas_call x1, Pallas kernels, shards(): pl.pallas_call(kernel, out_shape=[jax.ShapeDtypeStruct(shape, f32)] * 2,...  102 us

profile of v4, /device:TPU:2, one launch (start us, length us, event | category | flops | bytes accessed | tf_op | source)
XLA Modules:
  0.0 104.2 jit_solution(126189308085745095)
XLA Ops:
  0.6 101.6 %update.1 = (f32[32,4,4,1024]{3,2,1,0:T(4,128)S(1)}, f32[32,4,4,1024]{3,2,1,0:T(4,128)S(1)}) custom-call(f32[32,4,4,1024]{3,2,1,0:T(4,128)} %bitcast.5, f32[32,4,4,1024]{3,2,1,0:T(4,128)} %bitcast.6, f32[32,4,4,1024]{3,2,1,0:T(4,128)} %bitcast.7), custom_call_target="tpu_custom_call" | custom-call | tf_op jit(solution)/shard_map/update/pallas_call | solution.py:231
  102.2 2.0 %stored.1 = (f32[32,4,4,1024]{3,2,1,0:T(4,128)}, f32[32,4,4,1024]{3,2,1,0:T(4,128)}) custom-call(f32[32,4,4,1024]{3,2,1,0:T(4,128)S(1)} %get-tuple-element.6.a, f32[32,4,4,1024]{3,2,1,0:T(4,128)S(1)} %get-tuple-element.7.b), custom_call_target="tpu_custom_call" | custom-call | tf_op jit(solution)/shard_map/stored/pallas_call | solution.py:249

commit v5 on v4

--- a/solution.py
+++ b/solution.py
@@ -83,6 +83,14 @@
             return [planes[0] + ys[k] for k in range(1, YS)]
         return [planes[dz] + shifted[(k + (2 if dz > ZS // 2 else 0)) % YS] for k in range(YS)]
 
+    one, three = lax.rem(own_y + 1 + 2 * core, YS), lax.rem(own_y + 3 - 2 * core, YS)
+
+    def partners_home(dz):
+        if dz == 0:
+            return partners(0)
+        turn = [one, three] if dz <= ZS // 2 else [three, one]
+        return [planes[dz] + y for y in (ys[2], *turn, ys[0])]
+
     def load(dz):
         rows = pl.ds(planes[dz], YS)
         return [
@@ -185,9 +193,11 @@
             home[c, 2 * j] = first
             home[c, 2 * j + 1] = second
 
-        for dz in (0, 4, 5, 3, 6, 2, 7, 1):
-            for d in partners(dz):
-                send(home.at[c, d], back.at[c, me], home_send.at[c], home_recv.at[c], {"fsdp": d})
+        last = [planes[1] + own_y, planes[ZS - 1] + own_y]
+        order = [d for dz in (0, 4, 5, 3, 6, 2) for d in partners_home(dz)]
+        order += [d for pair in zip(partners_home(ZS - 1)[:3], partners_home(1)[:3]) for d in pair]
+        for d in order + last:
+            send(home.at[c, d], back.at[c, me], home_send.at[c], home_recv.at[c], {"fsdp": d})
         back[c, me] = home[c, me]
 
     load_w.wait()

time: 104 us -> 104 us (level)
  no operation moved by 1% of the time
where the time goes in v5:
time: 104 us
  Pallas kernels  103 us (99%)
    pallas_call x1, Pallas kernels, shards(): pl.pallas_call(kernel, out_shape=[jax.ShapeDtypeStruct(shape, f32)] * 2,...  101 us

profile of v5, /device:TPU:2, one launch (start us, length us, event | category | flops | bytes accessed | tf_op | source)
XLA Modules:
  0.0 103.7 jit_solution(3173437701876049268)
XLA Ops:
  0.6 101.0 %update.1 = (f32[32,4,4,1024]{3,2,1,0:T(4,128)S(1)}, f32[32,4,4,1024]{3,2,1,0:T(4,128)S(1)}) custom-call(f32[32,4,4,1024]{3,2,1,0:T(4,128)} %bitcast.5, f32[32,4,4,1024]{3,2,1,0:T(4,128)} %bitcast.6, f32[32,4,4,1024]{3,2,1,0:T(4,128)} %bitcast.7), custom_call_target="tpu_custom_call" | custom-call | tf_op jit(solution)/shard_map/update/pallas_call | solution.py:241
  101.7 2.0 %stored.1 = (f32[32,4,4,1024]{3,2,1,0:T(4,128)}, f32[32,4,4,1024]{3,2,1,0:T(4,128)}) custom-call(f32[32,4,4,1024]{3,2,1,0:T(4,128)S(1)} %get-tuple-element.6.a, f32[32,4,4,1024]{3,2,1,0:T(4,128)S(1)} %get-tuple-element.7.b), custom_call_target="tpu_custom_call" | custom-call | tf_op jit(solution)/shard_map/stored/pallas_call | solution.py:259

commit v6 on v5

--- a/solution.py
+++ b/solution.py
@@ -112,7 +112,7 @@
                 away[k // 2, d, pl.ds(4 * (k % 2), 4), :] = hold_rate * momentum + grad
 
     def send_away(c, dz):
-        for d in partners(dz):
+        for d in partners_home(dz):
             send(away.at[c, d], there.at[c, me], away_send.at[c], away_recv.at[c], {"fsdp": d})
 
     def tell(n):
@@ -193,23 +193,29 @@
             home[c, 2 * j] = first
             home[c, 2 * j + 1] = second
 
-        last = [planes[1] + own_y, planes[ZS - 1] + own_y]
-        order = [d for dz in (0, 4, 5, 3, 6, 2) for d in partners_home(dz)]
-        order += [d for pair in zip(partners_home(ZS - 1)[:3], partners_home(1)[:3]) for d in pair]
-        for d in order + last:
-            send(home.at[c, d], back.at[c, me], home_send.at[c], home_recv.at[c], {"fsdp": d})
+        far = [d for dz in (0, 4, 5, 3, 6, 2) for d in partners_home(dz)]
+        near = [d for pair in zip(partners_home(ZS - 1), partners_home(1)) for d in pair]
+        for part, devices in enumerate((far, near)):
+            for d in devices:
+                send(home.at[c, d], back.at[c, me], home_send.at[c], home_recv.at[c, part], {"fsdp": d})
         back[c, me] = home[c, me]
 
     load_w.wait()
-    for c in range(2):
-        wait(back.at[c, pl.ds(0, fsdp - 1)], home_recv.at[c])
-
-        @pl.loop(0, fsdp)
-        def _(d):
+    def update(c, dz):
+        @pl.loop(0, YS)
+        def _(y):
+            d = planes[dz] + y
             for k in range(2):
                 new_w[d, 2 * c + k] = (1.0 - learn_rate * decay_rate) * w[d, 2 * c + k] - learn_rate * back[
                     c, d, pl.ds(4 * k, 4), :
                 ]
+
+    for c in range(2):
+        for part, reached in enumerate(((0, 4, 5, 3, 6, 2), (ZS - 1, 1))):
+            messages = YS * len(reached) - (1 - part)
+            wait(back.at[c, pl.ds(0, messages)], home_recv.at[c, part])
+            for dz in reached:
+                update(c, dz)
 
     for c in range(2):
         wait(away.at[c, pl.ds(0, fsdp - 1)], away_send.at[c])
@@ -248,7 +254,7 @@
             pltpu.VMEM((2, rows, wide), f32),
             pltpu.VMEM((2, 2, rows, rows), f32),
             pltpu.VMEM((2, tp, 2, rows, rows), f32),
-            sem((ZS, 2)), sem, sem((2,)), sem((2,)), sem((2,)), sem((2,)), sem((2,)), sem((2,)),
+            sem((ZS, 2)), sem, sem((2,)), sem((2,)), sem((2,)), sem((2, 2)), sem((2,)), sem((2,)),
             pltpu.SemaphoreType.REGULAR((3,)),
         ],
         compiler_params=pltpu.CompilerParams(

time: 104 us -> 104 us (level)
  no operation moved by 1% of the time
where the time goes in v6:
time: 104 us
  Pallas kernels  103 us (99%)
    pallas_call x1, Pallas kernels, shards(): pl.pallas_call(kernel, out_shape=[jax.ShapeDtypeStruct(shape, f32)] * 2,...  101 us

profile of v6, /device:TPU:2, one launch (start us, length us, event | category | flops | bytes accessed | tf_op | source)
XLA Modules:
  0.0 103.5 jit_solution(17822491558672620598)
XLA Ops:
  0.6 100.9 %update.1 = (f32[32,4,4,1024]{3,2,1,0:T(4,128)S(1)}, f32[32,4,4,1024]{3,2,1,0:T(4,128)S(1)}) custom-call(f32[32,4,4,1024]{3,2,1,0:T(4,128)} %bitcast.5, f32[32,4,4,1024]{3,2,1,0:T(4,128)} %bitcast.6, f32[32,4,4,1024]{3,2,1,0:T(4,128)} %bitcast.7), custom_call_target="tpu_custom_call" | custom-call | tf_op jit(solution)/shard_map/update/pallas_call | solution.py:247
  101.5 2.0 %stored.1 = (f32[32,4,4,1024]{3,2,1,0:T(4,128)}, f32[32,4,4,1024]{3,2,1,0:T(4,128)}) custom-call(f32[32,4,4,1024]{3,2,1,0:T(4,128)S(1)} %get-tuple-element.6.a, f32[32,4,4,1024]{3,2,1,0:T(4,128)S(1)} %get-tuple-element.7.b), custom_call_target="tpu_custom_call" | custom-call | tf_op jit(solution)/shard_map/stored/pallas_call | solution.py:265

commit v7 on v6

--- a/solution.py
+++ b/solution.py
@@ -111,8 +111,12 @@
                 new_m[d, k] = momentum
                 away[k // 2, d, pl.ds(4 * (k % 2), 4), :] = hold_rate * momentum + grad
 
-    def send_away(c, dz):
-        for d in partners_home(dz):
+    def others(dz):
+        turn = 2 if dz > ZS // 2 else 0
+        return [planes[dz] + ys[1 + (k + turn) % 3] for k in range(3)]
+
+    def send_away(c, dz, devices=None):
+        for d in devices or partners_home(dz):
             send(away.at[c, d], there.at[c, me], away_send.at[c], away_recv.at[c], {"fsdp": d})
 
     def tell(n):
@@ -122,37 +126,40 @@
             )
 
     barrier = pltpu.get_barrier_semaphore()
-    for dz in (1, ZS - 1, 0):
-        for k in range(YS):
-            if dz or k:
-                pl.semaphore_signal(
-                    barrier, inc=1, device_id={"fsdp": planes[dz] + ys[k]}, device_id_type=MESH
-                )
+    for d in (planes[1] + own_y, planes[ZS - 1] + own_y, *partners(0)):
+        pl.semaphore_signal(barrier, inc=1, device_id={"fsdp": d}, device_id_type=MESH)
     for k in range(1, 4):
         pl.semaphore_signal(barrier, inc=1, device_id={"tp": lax.rem(col + k, tp)}, device_id_type=MESH)
 
-    for dz in OUTWARD:
+    for dz in OUTWARD[:2]:
         for copy in load(dz):
             copy.start()
-    for dz in (1, ZS - 1, 0):
+
+    pl.semaphore_wait(barrier, 2 + YS - 1 + tp - 1)
+    tell(0)
+    for dz in (1, ZS - 1):
         direct(dz)
-
-    pl.semaphore_wait(barrier, 3 * YS - 1 + tp - 1)
-    tell(0)
+        if dz == 1:
+            for far in OUTWARD[2:]:
+                for copy in load(far):
+                    copy.start()
+        for c in range(2):
+            send_away(c, dz, [planes[dz] + own_y])
+    pl.semaphore_wait(ready.at[0], 2)
+    tell(1)
     for c in range(2):
         for dz in (1, ZS - 1):
-            send_away(c, dz)
-        if c == 0:
-            send_away(c, 0)
-    for n in range(2):
-        for dz in (n + 2, ZS - 2 - n):
+            send_away(c, dz, others(dz))
+    direct(0)
+    send_away(0, 0)
+    for n in (2, 3):
+        pl.semaphore_wait(ready.at[n - 1], 2)
+        tell(n)
+        for dz in (n, ZS - n):
             direct(dz)
-        pl.semaphore_wait(ready.at[n], 2)
-        tell(n + 1)
-        for dz in (n + 2, ZS - 2 - n):
             send_away(0, dz)
+    pl.semaphore_wait(ready.at[3], 2)
     direct(4)
-    pl.semaphore_wait(ready.at[2], 2)
     send_away(0, 4)
     for dz in (4, 5, 3, 6, 2, 0):
         send_away(1, dz)
@@ -255,7 +262,7 @@
             pltpu.VMEM((2, 2, rows, rows), f32),
             pltpu.VMEM((2, tp, 2, rows, rows), f32),
             sem((ZS, 2)), sem, sem((2,)), sem((2,)), sem((2,)), sem((2, 2)), sem((2,)), sem((2,)),
-            pltpu.SemaphoreType.REGULAR((3,)),
+            pltpu.SemaphoreType.REGULAR((4,)),
         ],
         compiler_params=pltpu.CompilerParams(
             collective_id=0, has_side_effects=True, vmem_limit_bytes=48 * 1024 * 1024

time: 104 us -> 104 us (level)
  no operation moved by 1% of the time
where the time goes in v7:
time: 104 us; the launch traced here: 103 us
  Pallas kernels  103 us (99%)
    pallas_call x1, Pallas kernels, shards(): pl.pallas_call(kernel, out_shape=[jax.ShapeDtypeStruct(shape, f32)] * 2,...  101 us

profile of v7, /device:TPU:2, one launch (start us, length us, event | category | flops | bytes accessed | tf_op | source)
XLA Modules:
  0.0 103.4 jit_solution(5198927710601666531)
XLA Ops:
  0.6 100.7 %update.1 = (f32[32,4,4,1024]{3,2,1,0:T(4,128)S(1)}, f32[32,4,4,1024]{3,2,1,0:T(4,128)S(1)}) custom-call(f32[32,4,4,1024]{3,2,1,0:T(4,128)} %bitcast.5, f32[32,4,4,1024]{3,2,1,0:T(4,128)} %bitcast.6, f32[32,4,4,1024]{3,2,1,0:T(4,128)} %bitcast.7), custom_call_target="tpu_custom_call" | custom-call | tf_op jit(solution)/shard_map/update/pallas_call | solution.py:254
  101.3 2.0 %stored.1 = (f32[32,4,4,1024]{3,2,1,0:T(4,128)}, f32[32,4,4,1024]{3,2,1,0:T(4,128)}) custom-call(f32[32,4,4,1024]{3,2,1,0:T(4,128)S(1)} %get-tuple-element.6.a, f32[32,4,4,1024]{3,2,1,0:T(4,128)S(1)} %get-tuple-element.7.b), custom_call_target="tpu_custom_call" | custom-call | tf_op jit(solution)/shard_map/stored/pallas_call | solution.py:272
